TPU v7x, 32 devices: a whole 2x2x4 slice. The times are simulated.
32 devices in a mesh: leaf: 32 (over z, y, x, core).
Axes of the slice: x: 2, y: 2, z: 4, core: 2. Of those that a mesh axis runs over, the one named last changes fastest.
Arguments:
- coords: float32 [3, 262144], P(None, 'leaf'), may hold values from 0 to 1
- charges: bfloat16 [262144, 128], P('leaf'), may hold values from -6 to 6
- near_leaves: int32 [2048, 27], P('leaf'), may hold values from 0 to 191
- leaf_basis: bfloat16 [2048, 4096], P('leaf'), may hold values from -1 to 1
- leaf_transfer: bfloat16 [2048, 1024], P('leaf'), may hold values from -0.75 to 0.75
- mid_transfer: bfloat16 [256, 1024], P('leaf'), may hold values from -0.75 to 0.75
- base_transfer: bfloat16 [32, 1024], P('leaf'), may hold values from -0.75 to 0.75
- base_coupling: bfloat16 [6048, 1024], P('leaf'), may hold values from -0.01953125 to 0.01953125
- base_target: int32 [6048, 1], P('leaf'), may hold values from 0 to 31; in each aligned block of 189 rows (0 to 188, 189 to 377, ...) at most 11 rows name the same one
- base_source: int32 [6048], P('leaf'), may hold values from 0 to 31
- top_coupling: bfloat16 [256, 1024], P('leaf'), may hold values from -0.015625 to 0.015625
- top_target: int32 [256], P('leaf'), may hold values from 0 to 3
- top_source: int32 [256], P('leaf'), may hold values from 0 to 3
Outputs:
- potential: bfloat16 [262144, 128], P('leaf')
Inputs may be any that keep to these rules, and one draw needn't show every extreme that they name: `near_leaves`: entry j of leaf l names leaf 64 * (l // 64 - 1) + j: a leaf of the device before in Morton order, of the row's own device, or of the device after; repeats may occur. `base_target`: among the 189 blocks of one device no base cluster is the target more than 11 times; that count is reached.
All inputs are finite; a program needn't handle non-finite values.
Results may differ from a plain program's by a relative error of at most 0.01.
Values may be sent and summed in bfloat16 or wider, within the bound.
A program may use at most 128 MiB of HBM per device.

v0:
```python
import math

import jax
import jax.numpy as jnp
from jax import lax
from jax.sharding import PartitionSpec as P

K = 32
RHS = 128
M = 128
NB = 189


delta_sq = 0.0025


def extended(array, sides, width):
    for axis, dim in sides:
        size, length = (lax.axis_size(axis), array.shape[dim])
        up = [(i, (i + 1) % size) for i in range(size - 1)]
        down = [(j, i) for i, j in up]
        last = lax.slice_in_dim(array, length - width, length, axis=dim)
        first = lax.slice_in_dim(array, 0, width, axis=dim)
        before = lax.ppermute(last, axis, up)
        after = lax.ppermute(first, axis, down)
        array = jnp.concatenate([before, array, after], axis=dim)
    return array


def near_block(points, pool_points, pool_charges, columns):
    near_scale = 1.0 / math.sqrt(columns.shape[1] * points.shape[2])

    def near_step(running, column):
        other_points = jnp.take(pool_points, column, axis=1)
        other_charges = jnp.take(pool_charges, column, axis=0)
        squares = jnp.sum((points[:, :, :, None] - other_points[:, :, None, :]) ** 2, axis=0)
        kernel = (near_scale / jnp.sqrt(squares + delta_sq)).astype(jnp.bfloat16)
        update = jnp.einsum(
            "lab,lbr->lar", kernel, other_charges, preferred_element_type=jnp.float32
        )
        return (running + update, None)

    initial = jnp.zeros((points.shape[1], points.shape[2], pool_charges.shape[2]), jnp.float32)
    running, unused = lax.scan(near_step, initial, columns.T)
    return running


def per_device(
    coords,
    charges,
    near_leaves,
    leaf_basis,
    leaf_transfer,
    mid_transfer,
    base_transfer,
    base_coupling,
    base_target,
    base_source,
    top_coupling,
    top_target,
    top_source,
):
    single_precision = jnp.float32
    bf16 = jnp.bfloat16
    leaves = leaf_basis.shape[0]
    mid_count = leaves // 8
    base_count = leaves // 64
    devices = lax.axis_size("leaf")
    position = lax.axis_index("leaf")
    charge_row_block = charges.reshape(leaves, M, RHS)
    own_points = coords.reshape(3, leaves, M)
    point_rows = own_points.transpose(1, 0, 2).reshape(leaves, 3 * M)
    pool_points = (
        extended(point_rows, (("leaf", 0),), leaves).reshape(3 * leaves, 3, M).transpose(1, 0, 2)
    )
    pool_charges = extended(
        charge_row_block.reshape(leaves, M * RHS), (("leaf", 0),), leaves
    ).reshape(3 * leaves, M, RHS)
    basis_matrix = leaf_basis.reshape(leaves, K, M)
    leaf_coefficients = jnp.einsum(
        "xpt,xtu->xpu", basis_matrix, charge_row_block, preferred_element_type=single_precision
    ).astype(bf16)
    mid_coeffs = jnp.einsum(
        "mckp,mckr->mpr",
        leaf_transfer.reshape(mid_count, 8, K, K),
        leaf_coefficients.reshape(mid_count, 8, K, RHS),
        preferred_element_type=single_precision,
    ).astype(bf16)
    base_coeffs = jnp.einsum(
        "mckp,mckr->mpr",
        mid_transfer.reshape(base_count, 8, K, K),
        mid_coeffs.reshape(base_count, 8, K, RHS),
        preferred_element_type=single_precision,
    ).astype(bf16)
    base_lift = base_transfer.reshape(base_count, K, K)
    lifted = jnp.einsum(
        "bkp,bkr->bpr", base_lift, base_coeffs, preferred_element_type=single_precision
    ).astype(bf16)
    all_coeffs, all_lifted = (
        lax.all_gather(base_coeffs.reshape(base_count, K * RHS), "leaf", axis=0, tiled=True),
        lax.all_gather(lifted.reshape(base_count, K * RHS), "leaf", axis=0, tiled=True),
    )
    total_bases = base_count * devices
    total_tops = total_bases // 8
    every_base = all_coeffs.reshape(total_bases, K, RHS)
    top_coeffs = jnp.sum(
        all_lifted.reshape(total_tops, 8, K, RHS).astype(single_precision), axis=1
    ).astype(bf16)
    top_products = jnp.einsum(
        "bts,bsr->btr",
        top_coupling.reshape(-1, K, K),
        jnp.take(top_coeffs, top_source, axis=0),
        preferred_element_type=single_precision,
    )
    top_partial = jax.ops.segment_sum(top_products, top_target, num_segments=total_tops)
    top_sum = lax.psum(top_partial, "leaf")
    top_field = top_sum.astype(bf16)
    targets = base_target[:, 0]
    per_cluster = max(2, 2 * NB // devices)
    per_owner = per_cluster * base_count
    owners = targets // base_count
    onehot = (owners[:, None] == jnp.arange(devices, dtype=jnp.int32)[None, :]).astype(jnp.int32)
    earlier = jnp.cumsum(onehot, axis=0) - onehot
    slot_index = jnp.sum(earlier * onehot, axis=1)
    placed = owners * per_owner + slot_index
    send_blocks = jnp.zeros((devices * per_owner, K * K), bf16).at[placed].set(base_coupling)
    labels = base_source * base_count + (targets - owners * base_count)
    send_labels = jnp.full((devices * per_owner,), -1, jnp.int32).at[placed].set(labels)
    sent = (send_blocks.reshape(devices, per_owner, K * K), send_labels.reshape(devices, per_owner))
    blocks = lax.all_to_all(sent[0], "leaf", split_axis=0, concat_axis=0, tiled=True)
    got_labels = lax.all_to_all(sent[1], "leaf", split_axis=0, concat_axis=0, tiled=True)
    present = got_labels >= 0
    source_ids = jnp.where(present, got_labels // base_count, 0)
    gathered = jnp.take(every_base, source_ids, axis=0)
    shaped = blocks.reshape(blocks.shape[0], blocks.shape[1], K, K)
    result = jnp.einsum(
        "dnts,dnsr->dntr", shaped, gathered, preferred_element_type=single_precision
    )
    results, got_labels = (result, got_labels)
    local_ids = jnp.where(got_labels >= 0, got_labels % base_count, base_count).reshape(-1)
    coupled = jax.ops.segment_sum(results.reshape(-1, K, RHS), local_ids, num_segments=base_count)
    my_bases = position * base_count + jnp.arange(base_count, dtype=jnp.int32)
    top_mine = jnp.take(top_field, my_bases // 8, axis=0)
    base_field = (
        coupled
        + jnp.einsum("bkp,bpr->bkr", base_lift, top_mine, preferred_element_type=single_precision)
    ).astype(bf16)
    mid_field = jnp.einsum(
        "mkp,mpr->mkr",
        mid_transfer.reshape(mid_count, K, K),
        jnp.repeat(base_field, 8, axis=0),
        preferred_element_type=single_precision,
    ).astype(bf16)
    leaf_potential = jnp.einsum(
        "lkp,lpr->lkr",
        leaf_transfer.reshape(leaves, K, K),
        jnp.repeat(mid_field, 8, axis=0),
        preferred_element_type=single_precision,
    ).astype(bf16)
    near_field = near_block(own_points, pool_points, pool_charges, near_leaves)
    distant_field = jnp.einsum(
        "cbz,cbw->czw", basis_matrix, leaf_potential, preferred_element_type=single_precision
    )
    return (near_field + distant_field).astype(bf16).reshape(leaves * M, RHS)


def solution(mesh):
    in_specs = (
        P(None, "leaf"),
        P("leaf", None),
        P("leaf", None),
        P("leaf", None),
        P("leaf", None),
        P("leaf", None),
        P("leaf", None),
        P("leaf", None),
        P("leaf", None),
        P("leaf"),
        P("leaf", None),
        P("leaf"),
        P("leaf"),
    )
    out_specs = P("leaf", None)
    return jax.shard_map(
        per_device, mesh=mesh, in_specs=in_specs, out_specs=out_specs, check_vma=False
    )
```

profile of v0, /device:TPU:0, one launch (start us, length us, event | category | flops | bytes accessed | tf_op | source)
XLA Modules:
  0.0 797.9 jit_solution(6871703731802868991)
XLA Ops:
  21.0 8.4 %all-to-all-start = ((s32[32,1,11]{2,1,0:T(1,128)}), s32[32,1,11]{2,1,0:T(1,128)S(1)}, u32[]{:S(2)}, u32[]{:S(2)}) async-start(s32[32,1,11]{2,1,0:T(1,128)} %bitcast.22), calls=%async_computation | async-start | bytes 32768 | tf_op jit(solution)/shard_map/all_to_all | solution.py:131
  33.9 64.6 %all-gather = bf16[32,1,4096]{2,1,0:T(2,128)(2,1)S(1)} all-gather(bf16[1,1,4096]{2,1,0:T(2,128)(2,1)S(1)} %reshape.358), channel_id=1, replica_groups=mesh['leaf'=32] {'leaf'}, dimensions={0}, use_global_device_ids=true | all-gather | bytes 270336 | tf_op jit(solution)/shard_map/all_gather | solution.py:101
  102.0 38.0 %all-gather.1 = bf16[32,1,4096]{2,1,0:T(2,128)(2,1)S(1)} all-gather(bf16[1,1,4096]{2,1,0:T(2,128)(2,1)S(1)} %reshape.360), channel_id=1, replica_groups=mesh['leaf'=32] {'leaf'}, dimensions={0}, use_global_device_ids=true | all-gather | bytes 270336 | tf_op jit(solution)/shard_map/all_gather | solution.py:100
  158.2 41.0 %psum.7 = bf16[4,32,128]{2,1,0:T(8,128)(2,1)S(1)} all-reduce(f32[4,32,128]{2,1,0:T(8,128)S(1)} %scatter_fusion), channel_id=1, replica_groups=mesh['leaf'=32] {'leaf'}, use_global_device_ids=true, to_apply=%region_5.6 | all-reduce | flops 16384 | bytes 98304 | tf_op jit(solution)/shard_map/psum | solution.py:116
  219.2 31.1 %scatter_fusion.1 = f32[32,128,1]{1,0,2:T(8,128)S(1)} fusion(f32[32,128,1]{1,0,2:T(8,128)S(1)} %convolution_bitcast_fusion.2, s32[352]{0:T(512)S(1)} %reshape.354, f32[352,32,128]{2,1,0:T(8,128)} %bitcast.136), kind=kCustom, calls=%fused_computation.7 | custom fusion | flops 1441792 | bytes 17302912 | tf_op jit(solution)/shard_map/scatter-add | solution.py:141
  260.5 532.9 %while.12 = (s32[]{:T(128)}, f32[64,128,128]{2,1,0:T(8,128)}, f32[3,8192]{1,0:T(4,128)S(1)}, s32[27,64]{1,0:T(8,128)}, f32[3,192,128]{2,0,1:T(4,128)}, /*index=5*/bf16[192,128,128]{2,1,0:T(8,128)(2,1)}, s32[]{:T(128)}, s32[]{:T(128)}) while((s32[]{:T(128)}, f32[64,128,128]{2,1,0:T(8,128)}, f32[3,8192]{1,0:T(4,128)S(1)}, ...), condition=%wide.region_2.3_spmd.clone, body=%wide.region_0.2_spmd.clone.sunk | while | flops 283141696 | bytes 24057648 | solution.py:44
  292.3 6.6 select_add_fusion.2
  312.1 6.6 select_add_fusion.2
  331.8 6.6 select_add_fusion.2
  391.2 6.6 select_add_fusion.2
  411.0 6.6 select_add_fusion.2
  450.5 6.6 select_add_fusion.2
  470.3 6.6 select_add_fusion.2
  490.1 6.6 select_add_fusion.2
  529.7 6.6 select_add_fusion.2
  549.5 6.6 select_add_fusion.2
  569.2 6.6 select_add_fusion.2
  628.6 6.6 select_add_fusion.2
  648.4 6.6 select_add_fusion.2
  668.2 6.6 select_add_fusion.2
  687.9 6.6 select_add_fusion.2
  707.7 6.6 select_add_fusion.2
  727.5 6.6 select_add_fusion.2
  767.1 6.6 select_add_fusion.2
  (355 shorter events, 494.7 us)
Async XLA Ops:
  0.0 18.0 %copy-start.13 = (s32[189,1]{0,1:T(1,128)S(1)}, s32[189,1]{0,1:T(1,128)}, u32[]{:S(2)}) copy-start(s32[189,1]{0,1:T(1,128)} %param.23) | copy-start | bytes 2272
  0.0 29.5 %copy-start.7 = (bf16[64,4096]{1,0:T(8,128)(2,1)S(1)}, bf16[64,4096]{1,0:T(8,128)(2,1)}, u32[]{:S(2)}) copy-start(bf16[64,4096]{1,0:T(8,128)(2,1)} %param.18) | copy-start | bytes 1572868
  0.0 29.6 %copy-start.12 = (bf16[8,1024]{1,0:T(8,128)(2,1)S(1)}, bf16[8,1024]{1,0:T(8,128)(2,1)}, u32[]{:S(2)}) copy-start(bf16[8,1024]{1,0:T(8,128)(2,1)} %param.20) | copy-start | bytes 49156
  0.0 29.7 %copy-start.14 = (bf16[1,1024]{1,0:T(2,128)(2,1)S(1)}, bf16[1,1024]{1,0:T(2,128)(2,1)}, u32[]{:S(2)}) copy-start(bf16[1,1024]{1,0:T(2,128)(2,1)} %param.21) | copy-start | bytes 6148
  1.6 28.2 %copy-start.5 = (bf16[64,1024]{1,0:T(8,128)(2,1)S(1)}, bf16[64,1024]{1,0:T(8,128)(2,1)}, u32[]{:S(2)}) copy-start(bf16[64,1024]{1,0:T(8,128)(2,1)} %param.19) | copy-start | bytes 393220
  1.6 28.6 %copy-start = (bf16[8192,128]{1,0:T(8,128)(2,1)S(1)}, bf16[8192,128]{1,0:T(8,128)(2,1)}, u32[]{:S(2)}) copy-start(bf16[8192,128]{1,0:T(8,128)(2,1)} %param.16) | copy-start | bytes 6291460
  1.6 204.0 %collective-permute-start.1 = (f32[64,384]{1,0:T(8,128)}, f32[64,384]{1,0:T(8,128)}, u32[]{:S(2)}, u32[]{:S(2)}) collective-permute-start(f32[64,384]{1,0:T(8,128)} %bitcast.122), channel_id=1, source_target_pairs={{1,0},{2,1},{3,2},{4,3},{5,4},{6,5},{7,6},{8,7},{9,8},{10,9},{11,1... | collective-permute-start | bytes 294920 | tf_op jit(solution)/shard_map/ppermute | solution.py:25
  3.0 203.5 %collective-permute-start = (f32[64,384]{1,0:T(8,128)}, f32[64,384]{1,0:T(8,128)}, u32[]{:S(2)}, u32[]{:S(2)}) collective-permute-start(f32[64,384]{1,0:T(8,128)} %bitcast.122), channel_id=1, source_target_pairs={{0,1},{1,2},{2,3},{3,4},{4,5},{5,6},{6,7},{7,8},{8,9},{9,10},{10,1... | collective-permute-start | bytes 294920 | tf_op jit(solution)/shard_map/ppermute | solution.py:24
  10.9 240.2 %collective-permute-start.3 = (bf16[64,16384]{1,0:T(8,128)(2,1)}, bf16[64,16384]{1,0:T(8,128)(2,1)}, u32[]{:S(2)}, u32[]{:S(2)}) collective-permute-start(bf16[64,16384]{1,0:T(8,128)(2,1)} %reshape_reshape.3), channel_id=1, source_target_pairs={{1,0},{2,1},{3,2},{4,3},{5,4},{6,5},{7,6},{8,7},{9,8},{10,9},{11,1... | collective-permute-start | bytes 6291464 | tf_op jit(solution)/shard_map/ppermute | solution.py:25
  12.2 241.1 %collective-permute-start.2 = (bf16[64,16384]{1,0:T(8,128)(2,1)}, bf16[64,16384]{1,0:T(8,128)(2,1)}, u32[]{:S(2)}, u32[]{:S(2)}) collective-permute-start(bf16[64,16384]{1,0:T(8,128)(2,1)} %reshape_reshape.3), channel_id=1, source_target_pairs={{0,1},{1,2},{2,3},{3,4},{4,5},{5,6},{6,7},{7,8},{8,9},{9,10},{10,1... | collective-permute-start | bytes 6291464 | tf_op jit(solution)/shard_map/ppermute | solution.py:24
  19.0 14.2 %copy-start.15 = (s32[189,1]{0,1:T(1,128)}, s32[189,1]{0,1:T(1,128)S(1)}, u32[]{:S(2)}) copy-start(s32[189,1]{0,1:T(1,128)S(1)} %compare_select_fusion.7) | copy-start | bytes 2272
  21.0 124.0 %all-to-all-start = ((s32[32,1,11]{2,1,0:T(1,128)}), s32[32,1,11]{2,1,0:T(1,128)S(1)}, u32[]{:S(2)}, u32[]{:S(2)}) async-start(s32[32,1,11]{2,1,0:T(1,128)} %bitcast.22), calls=%async_computation | async-start | bytes 32768 | tf_op jit(solution)/shard_map/all_to_all | solution.py:131
  29.7 70.3 %copy-start.3 = (bf16[8,32,32]{2,1,0:T(8,128)(2,1)}, bf16[8,32,32]{2,1,0:T(8,128)(2,1)S(1)}, u32[]{:S(2)}) copy-start(bf16[8,32,32]{2,1,0:T(8,128)(2,1)S(1)} %reshape.231) | copy-start | bytes 49156
  29.8 3.3 copy-start.11
  33.1 0.6 copy-start.10
  100.0 49.0 %copy-start.6 = (bf16[64,1024]{1,0:T(8,128)(2,1)S(1)}, bf16[64,1024]{1,0:T(8,128)(2,1)}, u32[]{:S(2)}) copy-start(bf16[64,1024]{1,0:T(8,128)(2,1)} %param.19) | copy-start | bytes 393220
  145.1 8.8 %copy-start.9 = (s32[32,1,11]{2,1,0:T(1,128)}, s32[32,1,11]{2,1,0:T(1,128)S(1)}, u32[]{:S(2)}) copy-start(s32[32,1,11]{2,1,0:T(1,128)S(1)} %all-to-all-done) | copy-start | bytes 4228
  145.1 63.3 %all-to-all-start.1 = ((bf16[32,11,1024]{2,1,0:T(8,128)(2,1)}), bf16[32,11,1024]{2,1,0:T(8,128)(2,1)}, u32[]{:S(2)}, u32[]{:S(2)}) async-start(bf16[32,11,1024]{2,1,0:T(8,128)(2,1)} %reshape.239), calls=%async_computation.1 | async-start | bytes 2097152 | tf_op jit(solution)/shard_map/all_to_all | solution.py:130
  202.4 5.0 copy-start.1
  219.2 31.1 %copy-start.4 = (bf16[8,32,32]{2,1,0:T(8,128)(2,1)S(1)}, bf16[8,32,32]{2,1,0:T(8,128)(2,1)}, u32[]{:S(2)}) copy-start(bf16[8,32,32]{2,1,0:T(8,128)(2,1)} %copy-done.3) | copy-start | bytes 49156
  260.5 532.9 %copy-start.8 = (bf16[8,32,128]{2,1,0:T(8,128)(2,1)S(1)}, bf16[8,32,128]{2,1,0:T(8,128)(2,1)}, u32[]{:S(2)}) copy-start(bf16[8,32,128]{2,1,0:T(8,128)(2,1)} %fusion.15) | copy-start | bytes 196612
  260.5 533.0 %copy-start.2 = (bf16[64,32,32]{2,1,0:T(8,128)(2,1)S(1)}, bf16[64,32,32]{2,1,0:T(8,128)(2,1)}, u32[]{:S(2)}) copy-start(bf16[64,32,32]{2,1,0:T(8,128)(2,1)} %copy.43) | copy-start | bytes 393220
where the time goes:
time: 804 us; the launch traced here: 798 us
  other arithmetic  257 us (32%)
  matrix products  192 us (24%)
  local copies, waits for them, and re-layouts  180 us (22%)
  blocking collectives  144 us (18%)
  starting transfers between devices  24 us (3%)
    dot_general x27, matrix products, near_step(): jnp.einsum('lab,lbr->lar', kernel, other_charges, preferred_element_type=...  176 us
    reduce_sum x27, other arithmetic, near_step(): jnp.sum((points[:, :, :, None] - other_points[:, :, None, :]) ** 2, axis=0)  168 us
    gather x27, local copies, waits for them, and re-layouts, near_step(): other_charges = jnp.take(pool_charges, column, axis=0)  101 us
    all_gather x1, blocking collectives, per_device(): lax.all_gather(lifted.reshape(base_count, K * RHS), 'leaf', axis=0, tiled...  64.6 us
    gather x27, local copies, waits for them, and re-layouts, near_step(): other_points = jnp.take(pool_points, column, axis=1)  44.5 us
    psum x1, blocking collectives, per_device(): top_sum = lax.psum(top_partial, 'leaf')  41 us
    all_gather x1, blocking collectives, per_device(): lax.all_gather(base_coeffs.reshape(base_count, K * RHS), 'leaf', axis=0,...  38 us
    scatter-add x1, other arithmetic, per_device(): jax.ops.segment_sum(results.reshape(-1, K, RHS), local_ids, num_segments=...  31.1 us
  transfers between devices with their start and end apart: 6, of which 0 were waited for; matrix products, arithmetic and copies ran while one was open for 10% of the time, Pallas kernels for 0%

commit v1 on v0

v1 whole, which is shorter than its diff:
```python
import functools
import math

import jax
import jax.numpy as jnp
from jax import lax
from jax.experimental import pallas as pl
from jax.experimental.pallas import tpu as pltpu
from jax.sharding import PartitionSpec as P

K = 32
RHS = 128
M = 128
FEATURES = 32
DELTA_SQ = 0.0025

F32 = jnp.float32
BF16 = jnp.bfloat16
VMEM = pl.BlockSpec(memory_space=pltpu.VMEM)
SMEM = pl.BlockSpec(memory_space=pltpu.SMEM)
ANY = pl.BlockSpec(memory_space=pl.ANY)


def dot(a, b):
    return jnp.dot(a, b, preferred_element_type=F32)


def dot_ta(a, b):
    return lax.dot_general(a, b, (((0,), (0,)), ((), ())), preferred_element_type=F32)


def rows(index, size):
    return pl.ds(pl.multiple_of(index * size, size), size)


def pieces(x):
    high = lax.reduce_precision(x, 8, 7)
    rest = x - high
    middle = lax.reduce_precision(rest, 8, 7)
    return high, middle, lax.reduce_precision(rest - middle, 8, 7)


def split_points(coords, scale):
    x = (coords - 0.5) * scale
    h, m, l = pieces(x)
    return h, m, l, jnp.sum(x * x, axis=0, keepdims=True)


def target_features(coords, scale):
    h, m, l, norm = split_points(coords, scale)
    nh, nm, nl = pieces(norm + DELTA_SQ * scale * scale)
    ones = jnp.ones_like(norm)
    zeros = jnp.zeros((FEATURES - 24, coords.shape[1]), F32)
    return jnp.concatenate([h, h, m, h, l, m, nh, nm, nl, ones, ones, ones, zeros], axis=0)


def source_features(coords, scale):
    h, m, l, norm = split_points(coords, scale)
    nh, nm, nl = pieces(norm)
    ones = jnp.ones_like(norm)
    zeros = jnp.zeros((FEATURES - 24, coords.shape[1]), F32)
    h, m, l = -2.0 * h, -2.0 * m, -2.0 * l
    return jnp.concatenate(
        [h, m, h, l, h, m, ones, ones, ones, nh, nm, nl, zeros], axis=0
    ).astype(BF16)


def up_kernel(leaves, basis_ref, charges_ref, leaf_t_ref, mid_t_ref, base_t_ref, out_ref, coeffs):
    def group(i, carry):
        for j in range(8):
            leaf = i * 8 + j
            coeffs[rows(leaf, K), :] = dot(
                basis_ref[rows(leaf, K), :], charges_ref[rows(leaf, M), :]
            ).astype(BF16)
        return carry

    lax.fori_loop(0, leaves // 8, group, 0)
    mids = []
    for m in range(leaves // 8):
        part = slice(m * 8 * K, (m + 1) * 8 * K)
        mids.append(dot_ta(leaf_t_ref[part, :], coeffs[part, :]).astype(BF16))
    base = dot_ta(mid_t_ref[...], jnp.concatenate(mids, axis=0)).astype(BF16)
    out_ref[:K, :] = base
    out_ref[K:, :] = dot_ta(base_t_ref[...], base).astype(BF16)


def couple_kernel(
    devices, blocks, top_blocks, step,
    target_ref, source_ref, top_target_ref, top_source_ref,
    blocks_ref, top_blocks_ref, all_ref, out_ref, sums, top_coeffs, top_sums,
):
    sums[...] = jnp.zeros_like(sums)
    top_sums[...] = jnp.zeros_like(top_sums)
    for t in range(devices // 8):
        total = jnp.zeros((K, RHS), F32)
        for j in range(8):
            first = (t * 8 + j) * 2 * K + K
            total = total + all_ref[first : first + K, :].astype(F32)
        top_coeffs[t * K : (t + 1) * K, :] = total.astype(BF16)

    def group(i, carry):
        products = []
        for j in range(step):
            b = i * step + j
            products.append(
                dot(blocks_ref[rows(b, K), :], all_ref[rows(source_ref[b] * 2, K), :])
            )
        for j in range(step):
            where = rows(target_ref[i * step + j], K)
            sums[where, :] = sums[where, :] + products[j]
        return carry

    lax.fori_loop(0, blocks // step, group, 0)
    products = [
        dot(top_blocks_ref[b * K : (b + 1) * K, :], top_coeffs[rows(top_source_ref[b], K), :])
        for b in range(top_blocks)
    ]
    for b in range(top_blocks):
        where = rows(top_target_ref[b], K)
        top_sums[where, :] = top_sums[where, :] + products[b]
    for d in range(devices):
        out_ref[d * 2 * K : d * 2 * K + K, :] = sums[d * K : (d + 1) * K, :].astype(BF16)
        t = d // 8
        out_ref[d * 2 * K + K : (d + 1) * 2 * K, :] = top_sums[t * K : (t + 1) * K, :].astype(BF16)


def near_kernel(
    devices, leaves, named,
    near_ref, target_ref, source_ref, before_ref, own_ref, after_ref, got_ref,
    basis_ref, leaf_t_ref, mid_t_ref, base_t_ref, out_ref,
    pool, fields, even, odd, sems,
):
    points = leaves * M
    copies = [
        pltpu.make_async_copy(ref, pool.at[pl.ds(i * points, points), :], sems.at[i])
        for i, ref in enumerate((before_ref, own_ref, after_ref))
    ]
    for copy in copies:
        copy.start()

    total = jnp.sum(got_ref[...].astype(F32).reshape(devices, 2 * K, RHS), axis=0)
    base = (total[:K] + dot(base_t_ref[...], total[K:].astype(BF16))).astype(BF16)
    mid = dot(mid_t_ref[...], base).astype(BF16)
    for m in range(leaves // 8):
        part = slice(m * 8 * K, (m + 1) * 8 * K)
        fields[part, :] = dot(leaf_t_ref[part, :], mid[m * K : (m + 1) * K, :]).astype(BF16)

    groups = [range(j, min(j + 2, named)) for j in range(0, named, 2)]

    def make(leaf, kernel):
        mine = target_ref[:, rows(leaf, M)].T.astype(BF16)
        for group in groups:
            theirs = jnp.concatenate(
                [source_ref[:, rows(near_ref[leaf, j], M)] for j in group], axis=1
            )
            squares = dot(mine, theirs)
            kernel[:, group[0] * M : (group[-1] + 1) * M] = lax.rsqrt(squares.astype(BF16))

    def use(leaf, kernel):
        total = dot_ta(basis_ref[rows(leaf, K), :], fields[rows(leaf, K), :])
        for group in groups:
            theirs = jnp.concatenate([pool[rows(near_ref[leaf, j], M), :] for j in group], axis=0)
            total = total + dot(kernel[:, group[0] * M : (group[-1] + 1) * M], theirs)
        out_ref[rows(leaf, M), :] = total.astype(BF16)

    make(0, even)
    for copy in copies:
        copy.wait()

    def pair(i, carry):
        make(2 * i + 1, odd)
        use(2 * i, even)
        make(jnp.minimum(2 * i + 2, leaves - 1), even)
        use(2 * i + 1, odd)
        return carry

    lax.fori_loop(0, leaves // 2, pair, 0)


def per_device(
    coords,
    charges,
    near_leaves,
    leaf_basis,
    leaf_transfer,
    mid_transfer,
    base_transfer,
    base_coupling,
    base_target,
    base_source,
    top_coupling,
    top_target,
    top_source,
):
    leaves, named = near_leaves.shape
    devices = lax.axis_size("leaf")
    blocks, top_blocks = base_coupling.shape[0], top_coupling.shape[0]
    scale = math.sqrt(named * M)
    up = [(i, i + 1) for i in range(devices - 1)]
    down = [(i + 1, i) for i in range(devices - 1)]
    points_before = lax.ppermute(coords, "leaf", up)
    points_after = lax.ppermute(coords, "leaf", down)
    charges_before = lax.ppermute(charges, "leaf", up)
    charges_after = lax.ppermute(charges, "leaf", down)

    basis = leaf_basis.reshape(-1, M)
    leaf_t = leaf_transfer.reshape(-1, K)
    mid_t = mid_transfer.reshape(-1, K)
    base_t = base_transfer.reshape(-1, K)
    limit = pltpu.CompilerParams(vmem_limit_bytes=48 * 1024 * 1024)

    mine = pl.pallas_call(
        functools.partial(up_kernel, leaves),
        out_shape=jax.ShapeDtypeStruct((2 * K, RHS), BF16),
        in_specs=[VMEM] * 5,
        out_specs=VMEM,
        scratch_shapes=[pltpu.VMEM((leaves * K, RHS), BF16)],
        compiler_params=limit,
        cost_estimate=pl.CostEstimate(flops=70_000_000, bytes_accessed=3_000_000, transcendentals=0),
        name="upward",
    )(basis, charges, leaf_t, mid_t, base_t)
    gathered = lax.all_gather(mine, "leaf", axis=0, tiled=True)

    step = max(s for s in range(1, 33) if blocks % s == 0)
    partial = pl.pallas_call(
        functools.partial(couple_kernel, devices, blocks, top_blocks, step),
        out_shape=jax.ShapeDtypeStruct((devices * 2 * K, RHS), BF16),
        in_specs=[SMEM] * 4 + [VMEM] * 3,
        out_specs=VMEM,
        scratch_shapes=[
            pltpu.VMEM((devices * K, RHS), F32),
            pltpu.VMEM((devices // 8 * K, RHS), BF16),
            pltpu.VMEM((devices // 8 * K, RHS), F32),
        ],
        compiler_params=limit,
        cost_estimate=pl.CostEstimate(flops=50_000_000, bytes_accessed=3_000_000, transcendentals=0),
        name="couple",
    )(
        base_target[:, 0], base_source, top_target, top_source,
        base_coupling.reshape(-1, K), top_coupling.reshape(-1, K), gathered,
    )
    got = lax.all_to_all(partial, "leaf", split_axis=0, concat_axis=0, tiled=True)

    targets = target_features(coords, scale)
    sources = source_features(
        jnp.concatenate([points_before, coords, points_after], axis=1), scale
    )
    return pl.pallas_call(
        functools.partial(near_kernel, devices, leaves, named),
        out_shape=jax.ShapeDtypeStruct((leaves * M, RHS), BF16),
        in_specs=[SMEM, VMEM, VMEM, ANY, ANY, ANY] + [VMEM] * 5,
        out_specs=VMEM,
        scratch_shapes=[
            pltpu.VMEM((3 * leaves * M, RHS), BF16),
            pltpu.VMEM((leaves * K, RHS), BF16),
            pltpu.VMEM((M, named * M), BF16),
            pltpu.VMEM((M, named * M), BF16),
            pltpu.SemaphoreType.DMA((3,)),
        ],
        compiler_params=limit,
        cost_estimate=pl.CostEstimate(
            flops=8_000_000_000, bytes_accessed=12_000_000, transcendentals=28_000_000
        ),
        name="near",
    )(
        near_leaves, targets, sources, charges_before, charges, charges_after, got,
        basis, leaf_t, mid_t, base_t,
    )


def solution(mesh):
    split, flat = P("leaf", None), P("leaf")
    in_specs = (P(None, "leaf"),) + (split,) * 8 + (flat, split, flat, flat)
    return jax.shard_map(
        per_device, mesh=mesh, in_specs=in_specs, out_specs=split, check_vma=False
    )
```

time: 804 us -> 176 us (0.22)
  other arithmetic: 257 us -> 4.63 us
  matrix products: 192 us -> 0 us
  local copies, waits for them, and re-layouts: 180 us -> 36.2 us
  blocking collectives: 144 us -> 69.9 us
  Pallas kernels: 0 us -> 48.5 us
  starting transfers between devices: 24 us -> 14.7 us
    dot_general x35 -> x0, matrix products: 192 us -> none  [the longest x27 176 us: near_step(): jnp.einsum('lab,lbr->lar', kernel, other_charges, preferred_element_type=...]
    reduce_sum x29 -> x2, other arithmetic: 169 us -> 2.24 us  [split_points(): return (h, m, l, jnp.sum(x * x, axis=0, keepdims=True))]
    gather x56 -> x0, local copies, waits for them, and re-layouts: 150 us -> none  [the longest x27 101 us: near_step(): other_charges = jnp.take(pool_charges, column, axis=0)]
    pallas_call x0 -> x3, Pallas kernels: none -> 48.5 us  [the longest x1 43.1 us: per_device(): pl.pallas_call(functools.partial(near_kernel, devices, leaves, named), ou...]
    psum x1 -> x0, blocking collectives: 41 us -> none  [per_device(): top_sum = lax.psum(top_partial, 'leaf')]
    all_gather x2 -> x1, blocking collectives: 103 us -> 69.9 us  [per_device(): gathered = lax.all_gather(mine, 'leaf', axis=0, tiled=True)]
    scatter-add x2 -> x0, other arithmetic: 32 us -> none  [the longest x1 31.1 us: per_device(): jax.ops.segment_sum(results.reshape(-1, K, RHS), local_ids, num_segments=...]
    concatenate x2 -> x4, local copies, waits for them, and re-layouts: 1.86 us -> 26.5 us  [the longest x2 23.5 us: source_features(): jnp.concatenate([h, m, h, l, h, m, ones, ones, ones, nh, nm, nl, zeros],...]
  transfers between devices with their start and end apart: 6 -> 5, of which waited for: 0 -> 0; matrix products, arithmetic and copies ran while one was open for 10% -> 22% of each run, Pallas kernels for 0% -> 3%
where the time goes in v1:
time: 176 us; the launch traced here: 174 us
  blocking collectives  69.9 us (40%)
  Pallas kernels  48.5 us (28%)
  local copies, waits for them, and re-layouts  36.2 us (21%)
  starting transfers between devices  14.7 us (8%)
  other arithmetic  4.63 us (3%)
    all_gather x1, blocking collectives, per_device(): gathered = lax.all_gather(mine, 'leaf', axis=0, tiled=True)  69.9 us
    pallas_call x1, Pallas kernels, per_device(): pl.pallas_call(functools.partial(near_kernel, devices, leaves, named), ou...  43.1 us
    concatenate x2, local copies, waits for them, and re-layouts, source_features(): jnp.concatenate([h, m, h, l, h, m, ones, ones, ones, nh, nm, nl, zeros],...  23.5 us
    ppermute x1, starting transfers between devices, per_device(): charges_before = lax.ppermute(charges, 'leaf', up)  6.46 us
  transfers between devices with their start and end apart: 5, of which 0 were waited for; matrix products, arithmetic and copies ran while one was open for 22% of the time, Pallas kernels for 3%

profile of v1, /device:TPU:0, one launch (start us, length us, event | category | flops | bytes accessed | tf_op | source)
XLA Modules:
  0.0 174.1 jit_solution(9141987733093015187)
XLA Ops:
  0.0 3.1 %collective-permute-start = (f32[3,8192]{1,0:T(4,128)}, f32[3,8192]{1,0:T(4,128)}, u32[]{:S(2)}, u32[]{:S(2)}) collective-permute-start(f32[3,8192]{1,0:T(4,128)} %param.13), channel_id=1, source_target_pairs={{0,1},{1,2},{2,3},{3,4},{4,5},{5,6},{6,7},{7,8},{8,9},{9,10},{10,1... | collective-permute-start | bytes 294920 | tf_op jit(solution)/shard_map/ppermute | solution.py:201
  3.1 1.3 collective-permute-start.1
  4.4 1.3 collective-permute-start.3
  5.7 6.5 %collective-permute-start.2 = (bf16[8192,128]{1,0:T(8,128)(2,1)}, bf16[8192,128]{1,0:T(8,128)(2,1)}, u32[]{:S(2)}, u32[]{:S(2)}) collective-permute-start(bf16[8192,128]{1,0:T(8,128)(2,1)} %own_ref.1), channel_id=1, source_target_pairs={{0,1},{1,2},{2,3},{3,4},{4,5},{5,6},{6,7},{7,8},{8,9},{9,10},{10,1... | collective-permute-start | bytes 6291464 | tf_op jit(solution)/shard_map/ppermute | solution.py:203
  12.1 0.7 reduce
  12.9 0.8 reshape.94.mid_t_ref
  13.7 0.8 reshape.91.top_blocks_ref
  14.6 1.3 reshape.92.basis_ref
  15.9 1.3 reshape.93.leaf_t_ref
  17.2 1.6 copy-done
  18.8 2.0 %upward.1 = bf16[64,128]{1,0:T(8,128)(2,1)S(1)} custom-call(bf16[2048,128]{1,0:T(8,128)(2,1)S(1)} %reshape.92.basis_ref, bf16[8192,128]{1,0:T(8,128)(2,1)S(1)} %copy-done, bf16[2048,32]{1,0:T(8,128)(2,1)S(1)} %reshape.93.leaf_t_ref, bf16[256,32]{1,0:T(8,128)(2,1)S(1)} %reshape.94.mid_t_ref, bf16[32,32]{1,0:T(8,128)(2,1)S(1)} %reshape.95.base_t_ref), custom_call_target="tpu_custom_call" | custom-call | flops 70000000 | bytes 3000000 | tf_op jit(solution)/shard_map/upward/pallas_call | solution.py:212
  20.8 69.9 %all_gather.3.all_ref = bf16[2048,128]{1,0:T(8,128)(2,1)S(1)} all-gather(bf16[64,128]{1,0:T(8,128)(2,1)S(1)} %upward.1), channel_id=1, replica_groups=mesh['leaf'=32] {'leaf'}, dimensions={0}, use_global_device_ids=true | all-gather | bytes 540672 | tf_op jit(solution)/shard_map/all_gather | solution.py:222
  90.7 2.2 %reshape.90.blocks_ref = bf16[6048,32]{1,0:T(8,128)(2,1)S(1)} reshape(bf16[189,1024]{1,0:T(8,128)(2,1)} %param.20) | data formatting | bytes 774144 | tf_op jit(solution)/shard_map/reshape | solution.py:240
  93.0 3.5 %couple.1 = bf16[2048,128]{1,0:T(8,128)(2,1)} custom-call(s32[189]{0:T(256)S(1)} %bitcast.6, s32[189]{0:T(256)S(1)} %copy-done.3, s32[8]{0:T(128)S(1)} %copy-done.4, s32[8]{0:T(128)S(1)} %copy-done.5, bf16[6048,32]{1,0:T(8,128)(2,1)S(1)} %reshape.90.blocks_ref, bf16[256,32]{1,0:T(8,128)(2,1)S(1)} %reshape.91.top_blocks_ref, ...), custom_call_target="tpu_custom_call" | custom-call | flops 50000000 | bytes 3000000 | tf_op jit(solution)/shard_map/couple/pallas_call | solution.py:225
  96.5 2.6 %all-to-all-start = ((bf16[32,64,128]{2,1,0:T(8,128)(2,1)}), bf16[32,64,128]{2,1,0:T(8,128)(2,1)S(1)}, u32[]{:S(2)}, u32[]{:S(2)}) async-start(bf16[32,64,128]{2,1,0:T(8,128)(2,1)} %bitcast.3), calls=%async_computation | async-start | bytes 1048576 | tf_op jit(solution)/shard_map/all_to_all | solution.py:242
  99.2 0.7 subtract_reduce-precision_fusion.1
  100.0 0.7 concatenate.16
  100.7 2.3 %concatenate.17.target_ref = f32[32,8192]{1,0:T(8,128)S(1)} concatenate(f32[3,8192]{1,0:T(4,128)S(1)} %get-tuple-element.12, f32[3,8192]{1,0:T(4,128)S(1)} %get-tuple-element.12, f32[3,8192]{1,0:T(4,128)S(1)} %get-tuple-element.11, f32[3,8192]{1,0:T(4,128)S(1)} %get-tuple-element.12, f32[3,8192]{1,0:T(4,128)S(1)} %get-tuple-element.10, f32[3,8192]{1,0:T(4,128)S(1)} %get-tuple-element.11, ...), dimensions={0} | concatenate | bytes 2097152 | tf_op jit(solution)/shard_map/concatenate | solution.py:54
  103.0 2.1 %multiply_reduce_fusion = (f32[24576]{0:T(1024)S(1)}, bf16[3,24576]{1,0:T(4,128)(2,1)S(1)}, bf16[3,24576]{1,0:T(4,128)(2,1)}, bf16[3,24576]{1,0:T(4,128)(2,1)S(1)}) fusion(f32[3,8192]{1,0:T(4,128)} %collective-permute-done.1, f32[3,8192]{1,0:T(4,128)S(1)} %copy-done.6, f32[3,8192]{1,0:T(4,128)} %collective-permute-done), kind=kLoop, calls=%fused_computation.11 | loop fusion | flops 1228800 | bytes 835584 | tf_op jit(solution)/shard_map/reduce_sum | solution.py:46
  105.1 1.0 fusion.7
  106.1 0.7 concatenate.19
  106.8 22.8 %concatenate.20.source_ref = bf16[32,24576]{1,0:T(8,128)(2,1)} concatenate(bf16[3,24576]{1,0:T(4,128)(2,1)S(1)} %get-tuple-element.8, bf16[3,24576]{1,0:T(4,128)(2,1)S(1)} %get-tuple-element.6, bf16[3,24576]{1,0:T(4,128)(2,1)S(1)} %get-tuple-element.8, bf16[3,24576]{1,0:T(4,128)(2,1)} %get-tuple-element.7, bf16[3,24576]{1,0:T(4,128)(2,1)S(1)} %get-tuple-element.8, ...), dimensions={0} | concatenate | bytes 3145728 | tf_op jit(solution)/shard_map/concatenate | solution.py:63
  129.7 1.4 copy-done.1
  131.1 43.1 %near.1 = bf16[8192,128]{1,0:T(8,128)(2,1)} custom-call(s32[64,27]{1,0:T(8,128)S(1)} %copy.15.near_ref, f32[32,8192]{1,0:T(8,128)S(1)} %concatenate.17.target_ref, bf16[32,24576]{1,0:T(8,128)(2,1)S(1)} %copy-done.1, bf16[8192,128]{1,0:T(8,128)(2,1)} %collective-permute-done.2.before_ref, bf16[8192,128]{1,0:T(8,128)(2,1)} %own_ref.1, ...), custom_call_target="tpu_custom_call" | custom-call | flops 8000000000 | bytes 12000000 | tf_op jit(solution)/shard_map/near/pallas_call | solution.py:248
  (25 shorter events, 0.4 us)
Async XLA Ops:
  0.0 103.0 %collective-permute-start = (f32[3,8192]{1,0:T(4,128)}, f32[3,8192]{1,0:T(4,128)}, u32[]{:S(2)}, u32[]{:S(2)}) collective-permute-start(f32[3,8192]{1,0:T(4,128)} %param.13), channel_id=1, source_target_pairs={{0,1},{1,2},{2,3},{3,4},{4,5},{5,6},{6,7},{7,8},{8,9},{9,10},{10,1... | collective-permute-start | bytes 294920 | tf_op jit(solution)/shard_map/ppermute | solution.py:201
  3.1 99.9 %collective-permute-start.1 = (f32[3,8192]{1,0:T(4,128)}, f32[3,8192]{1,0:T(4,128)}, u32[]{:S(2)}, u32[]{:S(2)}) collective-permute-start(f32[3,8192]{1,0:T(4,128)} %param.13), channel_id=1, source_target_pairs={{1,0},{2,1},{3,2},{4,3},{5,4},{6,5},{7,6},{8,7},{9,8},{10,9},{11,1... | collective-permute-start | bytes 294920 | tf_op jit(solution)/shard_map/ppermute | solution.py:202
  4.4 125.3 %collective-permute-start.3 = (bf16[8192,128]{1,0:T(8,128)(2,1)}, bf16[8192,128]{1,0:T(8,128)(2,1)}, u32[]{:S(2)}, u32[]{:S(2)}) collective-permute-start(bf16[8192,128]{1,0:T(8,128)(2,1)} %own_ref.1), channel_id=1, source_target_pairs={{1,0},{2,1},{3,2},{4,3},{5,4},{6,5},{7,6},{8,7},{9,8},{10,9},{11,1... | collective-permute-start | bytes 6291464 | tf_op jit(solution)/shard_map/ppermute | solution.py:204
  5.7 124.0 %collective-permute-start.2 = (bf16[8192,128]{1,0:T(8,128)(2,1)}, bf16[8192,128]{1,0:T(8,128)(2,1)}, u32[]{:S(2)}, u32[]{:S(2)}) collective-permute-start(bf16[8192,128]{1,0:T(8,128)(2,1)} %own_ref.1), channel_id=1, source_target_pairs={{0,1},{1,2},{2,3},{3,4},{4,5},{5,6},{6,7},{7,8},{8,9},{9,10},{10,1... | collective-permute-start | bytes 6291464 | tf_op jit(solution)/shard_map/ppermute | solution.py:203
  17.2 1.6 copy-start
  18.8 74.2 %copy-start.2 = (s32[189,1]{0,1:T(1,128)S(1)}, s32[189,1]{0,1:T(1,128)}, u32[]{:S(2)}) copy-start(s32[189,1]{0,1:T(1,128)} %param.21) | copy-start | bytes 2272
  18.8 74.2 %copy-start.3 = (s32[189]{0:T(256)S(1)}, s32[189]{0:T(256)}, u32[]{:S(2)}) copy-start(s32[189]{0:T(256)} %source_ref.1) | copy-start | bytes 2272
  18.8 74.2 %copy-start.4 = (s32[8]{0:T(128)S(1)}, s32[8]{0:T(128)}, u32[]{:S(2)}) copy-start(s32[8]{0:T(128)} %top_target_ref.1) | copy-start | bytes 100
  18.8 74.2 %copy-start.5 = (s32[8]{0:T(128)S(1)}, s32[8]{0:T(128)}, u32[]{:S(2)}) copy-start(s32[8]{0:T(128)} %top_source_ref.1) | copy-start | bytes 100
  92.9 6.1 %copy-start.6 = (f32[3,8192]{1,0:T(4,128)S(1)}, f32[3,8192]{1,0:T(4,128)}, u32[]{:S(2)}) copy-start(f32[3,8192]{1,0:T(4,128)} %param.13) | copy-start | bytes 294916
  93.0 7.0 %copy-start.7 = (s32[64,27]{0,1:T(8,128)S(1)}, s32[64,27]{0,1:T(8,128)}, u32[]{:S(2)}) copy-start(s32[64,27]{0,1:T(8,128)} %param.15) | copy-start | bytes 20740
  96.5 33.2 %all-to-all-start = ((bf16[32,64,128]{2,1,0:T(8,128)(2,1)}), bf16[32,64,128]{2,1,0:T(8,128)(2,1)S(1)}, u32[]{:S(2)}, u32[]{:S(2)}) async-start(bf16[32,64,128]{2,1,0:T(8,128)(2,1)} %bitcast.3), calls=%async_computation | async-start | bytes 1048576 | tf_op jit(solution)/shard_map/all_to_all | solution.py:242
  129.7 1.4 copy-start.1

commit v2 on v1

--- a/solution.py
+++ b/solution.py
@@ -34,35 +34,17 @@
 
 
 def pieces(x):
-    high = lax.reduce_precision(x, 8, 7)
+    high = x.astype(BF16).astype(F32)
     rest = x - high
-    middle = lax.reduce_precision(rest, 8, 7)
-    return high, middle, lax.reduce_precision(rest - middle, 8, 7)
-
-
-def split_points(coords, scale):
-    x = (coords - 0.5) * scale
-    h, m, l = pieces(x)
-    return h, m, l, jnp.sum(x * x, axis=0, keepdims=True)
-
-
-def target_features(coords, scale):
-    h, m, l, norm = split_points(coords, scale)
-    nh, nm, nl = pieces(norm + DELTA_SQ * scale * scale)
-    ones = jnp.ones_like(norm)
-    zeros = jnp.zeros((FEATURES - 24, coords.shape[1]), F32)
-    return jnp.concatenate([h, h, m, h, l, m, nh, nm, nl, ones, ones, ones, zeros], axis=0)
-
-
-def source_features(coords, scale):
-    h, m, l, norm = split_points(coords, scale)
-    nh, nm, nl = pieces(norm)
-    ones = jnp.ones_like(norm)
-    zeros = jnp.zeros((FEATURES - 24, coords.shape[1]), F32)
-    h, m, l = -2.0 * h, -2.0 * m, -2.0 * l
-    return jnp.concatenate(
-        [h, m, h, l, h, m, ones, ones, ones, nh, nm, nl, zeros], axis=0
-    ).astype(BF16)
+    middle = rest.astype(BF16).astype(F32)
+    return high, middle, (rest - middle).astype(BF16).astype(F32)
+
+
+def write_features(rows_ref, first, width, parts):
+    at = 0
+    for part in parts:
+        rows_ref[at : at + part.shape[0], pl.ds(first, width)] = part
+        at += part.shape[0]
 
 
 def up_kernel(leaves, basis_ref, charges_ref, leaf_t_ref, mid_t_ref, base_t_ref, out_ref, coeffs):
@@ -124,57 +106,82 @@
         out_ref[d * 2 * K + K : (d + 1) * 2 * K, :] = top_sums[t * K : (t + 1) * K, :].astype(BF16)
 
 
-def near_kernel(
-    devices, leaves, named,
-    near_ref, target_ref, source_ref, before_ref, own_ref, after_ref, got_ref,
-    basis_ref, leaf_t_ref, mid_t_ref, base_t_ref, out_ref,
-    pool, fields, even, odd, sems,
+def groups_of(named):
+    return [range(j, min(j + 2, named)) for j in range(0, named, 2)]
+
+
+def make_kernel(
+    leaves, named, scale, width,
+    near_ref, before_ref, own_ref, after_ref, out_ref, targets, staged, sources,
 ):
     points = leaves * M
-    copies = [
-        pltpu.make_async_copy(ref, pool.at[pl.ds(i * points, points), :], sems.at[i])
-        for i, ref in enumerate((before_ref, own_ref, after_ref))
-    ]
-    for copy in copies:
-        copy.start()
-
-    total = jnp.sum(got_ref[...].astype(F32).reshape(devices, 2 * K, RHS), axis=0)
-    base = (total[:K] + dot(base_t_ref[...], total[K:].astype(BF16))).astype(BF16)
-    mid = dot(mid_t_ref[...], base).astype(BF16)
-    for m in range(leaves // 8):
-        part = slice(m * 8 * K, (m + 1) * 8 * K)
-        fields[part, :] = dot(leaf_t_ref[part, :], mid[m * K : (m + 1) * K, :]).astype(BF16)
-
-    groups = [range(j, min(j + 2, named)) for j in range(0, named, 2)]
-
-    def make(leaf, kernel):
-        mine = target_ref[:, rows(leaf, M)].T.astype(BF16)
-        for group in groups:
+
+    @pl.when(pl.program_id(0) == 0)
+    def _():
+        for place, ref in enumerate((before_ref, own_ref, after_ref)):
+
+            def chunk(i, carry, place=place, ref=ref):
+                first = pl.multiple_of(i * width, width)
+                x = (ref[:, pl.ds(first, width)] - 0.5) * scale
+                h, m, l = pieces(x)
+                norm = x[0:1] * x[0:1] + x[1:2] * x[1:2] + x[2:3] * x[2:3]
+                ones = jnp.ones((3, width), F32)
+                zeros = jnp.zeros((FEATURES - 24, width), F32)
+                if place == 1:
+                    n = pieces(norm + DELTA_SQ * scale * scale)
+                    write_features(targets, first, width, [h, h, m, h, l, m, *n, ones, zeros])
+                n = pieces(norm)
+                h, m, l = -2.0 * h, -2.0 * m, -2.0 * l
+                write_features(staged, 0, width, [h, m, h, l, h, m, ones, *n, zeros])
+                where = pl.ds(pl.multiple_of(place * points + first, width), width)
+                sources[:, where] = staged[...].astype(BF16)
+                return carry
+
+            lax.fori_loop(0, points // width, chunk, 0)
+
+    for k in range(out_ref.shape[0]):
+        leaf = pl.program_id(0) * out_ref.shape[0] + k
+        mine = targets[:, rows(leaf, M)].T.astype(BF16)
+        for group in groups_of(named):
             theirs = jnp.concatenate(
-                [source_ref[:, rows(near_ref[leaf, j], M)] for j in group], axis=1
+                [sources[:, rows(near_ref[leaf, j], M)] for j in group], axis=1
             )
             squares = dot(mine, theirs)
-            kernel[:, group[0] * M : (group[-1] + 1) * M] = lax.rsqrt(squares.astype(BF16))
-
-    def use(leaf, kernel):
+            out_ref[k, :, group[0] * M : (group[-1] + 1) * M] = lax.rsqrt(squares.astype(BF16))
+
+
+def use_kernel(
+    devices, leaves, named,
+    near_ref, kernel_ref, before_ref, own_ref, after_ref, got_ref,
+    basis_ref, leaf_t_ref, mid_t_ref, base_t_ref, out_ref,
+    pool, fields, sems,
+):
+    points = leaves * M
+
+    @pl.when(pl.program_id(0) == 0)
+    def _():
+        copies = [
+            pltpu.make_async_copy(ref, pool.at[pl.ds(i * points, points), :], sems.at[i])
+            for i, ref in enumerate((before_ref, own_ref, after_ref))
+        ]
+        for copy in copies:
+            copy.start()
+        total = jnp.sum(got_ref[...].astype(F32).reshape(devices, 2 * K, RHS), axis=0)
+        base = (total[:K] + dot(base_t_ref[...], total[K:].astype(BF16))).astype(BF16)
+        mid = dot(mid_t_ref[...], base).astype(BF16)
+        for m in range(leaves // 8):
+            part = slice(m * 8 * K, (m + 1) * 8 * K)
+            fields[part, :] = dot(leaf_t_ref[part, :], mid[m * K : (m + 1) * K, :]).astype(BF16)
+        for copy in copies:
+            copy.wait()
+
+    for k in range(kernel_ref.shape[0]):
+        leaf = pl.program_id(0) * kernel_ref.shape[0] + k
         total = dot_ta(basis_ref[rows(leaf, K), :], fields[rows(leaf, K), :])
-        for group in groups:
+        for group in groups_of(named):
             theirs = jnp.concatenate([pool[rows(near_ref[leaf, j], M), :] for j in group], axis=0)
-            total = total + dot(kernel[:, group[0] * M : (group[-1] + 1) * M], theirs)
-        out_ref[rows(leaf, M), :] = total.astype(BF16)
-
-    make(0, even)
-    for copy in copies:
-        copy.wait()
-
-    def pair(i, carry):
-        make(2 * i + 1, odd)
-        use(2 * i, even)
-        make(jnp.minimum(2 * i + 2, leaves - 1), even)
-        use(2 * i + 1, odd)
-        return carry
-
-    lax.fori_loop(0, leaves // 2, pair, 0)
+            total = total + dot(kernel_ref[k, :, group[0] * M : (group[-1] + 1) * M], theirs)
+        out_ref[k * M : (k + 1) * M, :] = total.astype(BF16)
 
 
 def per_device(
@@ -200,8 +207,6 @@
     down = [(i + 1, i) for i in range(devices - 1)]
     points_before = lax.ppermute(coords, "leaf", up)
     points_after = lax.ppermute(coords, "leaf", down)
-    charges_before = lax.ppermute(charges, "leaf", up)
-    charges_after = lax.ppermute(charges, "leaf", down)
 
     basis = leaf_basis.reshape(-1, M)
     leaf_t = leaf_transfer.reshape(-1, K)
@@ -220,6 +225,11 @@
         name="upward",
     )(basis, charges, leaf_t, mid_t, base_t)
     gathered = lax.all_gather(mine, "leaf", axis=0, tiled=True)
+    gathered, outgoing, points_before, points_after = lax.optimization_barrier(
+        (gathered, charges, points_before, points_after)
+    )
+    charges_before = lax.ppermute(outgoing, "leaf", up)
+    charges_after = lax.ppermute(outgoing, "leaf", down)
 
     step = max(s for s in range(1, 33) if blocks % s == 0)
     partial = pl.pallas_call(
@@ -241,29 +251,45 @@
     )
     got = lax.all_to_all(partial, "leaf", split_axis=0, concat_axis=0, tiled=True)
 
-    targets = target_features(coords, scale)
-    sources = source_features(
-        jnp.concatenate([points_before, coords, points_after], axis=1), scale
-    )
+    partial, points_before = lax.optimization_barrier((partial, points_before))
+    got = lax.all_to_all(partial, "leaf", split_axis=0, concat_axis=0, tiled=True)
+    each = 4
+    kernels = pl.pallas_call(
+        functools.partial(make_kernel, leaves, named, scale, 1024),
+        grid=(leaves // each,),
+        out_shape=jax.ShapeDtypeStruct((leaves, M, named * M), BF16),
+        in_specs=[SMEM, VMEM, VMEM, VMEM],
+        out_specs=pl.BlockSpec((each, M, named * M), lambda i: (i, 0, 0)),
+        scratch_shapes=[
+            pltpu.VMEM((FEATURES, leaves * M), F32),
+            pltpu.VMEM((FEATURES, 1024), F32),
+            pltpu.VMEM((FEATURES, 3 * leaves * M), BF16),
+        ],
+        compiler_params=limit,
+        cost_estimate=pl.CostEstimate(
+            flops=16_000_000_000, bytes_accessed=60_000_000, transcendentals=28_000_000
+        ),
+        name="make",
+    )(near_leaves, points_before, coords, points_after)
     return pl.pallas_call(
-        functools.partial(near_kernel, devices, leaves, named),
+        functools.partial(use_kernel, devices, leaves, named),
+        grid=(leaves // each,),
         out_shape=jax.ShapeDtypeStruct((leaves * M, RHS), BF16),
-        in_specs=[SMEM, VMEM, VMEM, ANY, ANY, ANY] + [VMEM] * 5,
-        out_specs=VMEM,
+        in_specs=[SMEM, pl.BlockSpec((each, M, named * M), lambda i: (i, 0, 0)), ANY, ANY, ANY]
+        + [VMEM] * 5,
+        out_specs=pl.BlockSpec((each * M, RHS), lambda i: (i, 0)),
         scratch_shapes=[
             pltpu.VMEM((3 * leaves * M, RHS), BF16),
             pltpu.VMEM((leaves * K, RHS), BF16),
-            pltpu.VMEM((M, named * M), BF16),
-            pltpu.VMEM((M, named * M), BF16),
             pltpu.SemaphoreType.DMA((3,)),
         ],
         compiler_params=limit,
         cost_estimate=pl.CostEstimate(
-            flops=8_000_000_000, bytes_accessed=12_000_000, transcendentals=28_000_000
+            flops=8_000_000_000, bytes_accessed=66_000_000, transcendentals=0
         ),
-        name="near",
+        name="use",
     )(
-        near_leaves, targets, sources, charges_before, charges, charges_after, got,
+        near_leaves, kernels, charges_before, charges, charges_after, got,
         basis, leaf_t, mid_t, base_t,
     )
 

time: 176 us -> 148 us (0.84)
  local copies, waits for them, and re-layouts: 36.2 us -> 9.88 us
  blocking collectives: 69.9 us -> 46.7 us
  Pallas kernels: 48.5 us -> 65.5 us
  waiting for transfers between devices: 0.01 us -> 11.9 us
  other arithmetic: 4.63 us -> 0.71 us
  starting transfers between devices: 14.7 us -> 12 us
    concatenate x4 -> x0, local copies, waits for them, and re-layouts: 26.5 us -> none  [the longest x2 23.5 us: source_features(): jnp.concatenate([h, m, h, l, h, m, ones, ones, ones, nh, nm, nl, zeros],...]
    all_gather x1, blocking collectives: 69.9 us -> 46.7 us  [per_device(): gathered = lax.all_gather(mine, 'leaf', axis=0, tiled=True)]
    pallas_call x1 -> x2, Pallas kernels: 43.1 us -> 59.3 us  [the longest x1 31.9 us: per_device(): pl.pallas_call(functools.partial(use_kernel, devices, leaves, named), gri...]
    all_to_all x1, waiting for transfers between devices: 0.01 us -> 11.9 us  [per_device(): lax.all_to_all(partial, 'leaf', split_axis=0, concat_axis=0, tiled=True)]
    reduce_sum x2 -> x0, other arithmetic: 2.24 us -> none  [split_points(): return (h, m, l, jnp.sum(x * x, axis=0, keepdims=True))]
    ppermute x2, starting transfers between devices: 7.75 us -> 5.66 us  [the longest x1 4.38 us: per_device(): charges_before = lax.ppermute(outgoing, 'leaf', up)]
    unnamed x17 -> x25, local copies, waits for them, and re-layouts: 3.11 us -> 4.04 us
  transfers between devices with their start and end apart: 5 -> 5, of which waited for: 0 -> 1; matrix products, arithmetic and copies ran while one was open for 22% -> 5% of each run, Pallas kernels for 3% -> 23%
where the time goes in v2:
time: 148 us; the launch traced here: 147 us
  Pallas kernels  65.5 us (44%)
  blocking collectives  46.7 us (32%)
  starting transfers between devices  12 us (8%)
  waiting for transfers between devices  11.9 us (8%)
  local copies, waits for them, and re-layouts  9.88 us (7%)
    all_gather x1, blocking collectives, per_device(): gathered = lax.all_gather(mine, 'leaf', axis=0, tiled=True)  46.7 us
    pallas_call x1, Pallas kernels, per_device(): pl.pallas_call(functools.partial(use_kernel, devices, leaves, named), gri...  31.9 us
    pallas_call x1, Pallas kernels, per_device(): pl.pallas_call(functools.partial(make_kernel, leaves, named, scale, 1024)...  27.4 us
    all_to_all x1, waiting for transfers between devices, per_device(): lax.all_to_all(partial, 'leaf', split_axis=0, concat_axis=0, tiled=True)  11.9 us
    ppermute x1, starting transfers between devices, per_device(): charges_before = lax.ppermute(outgoing, 'leaf', up)  4.38 us
    unnamed x25, local copies, waits for them, and re-layouts  4.04 us
    pallas_call x1, Pallas kernels, per_device(): pl.pallas_call(functools.partial(up_kernel, leaves), out_shape=jax.ShapeD...  3.56 us
  transfers between devices with their start and end apart: 5, of which 1 were waited for; matrix products, arithmetic and copies ran while one was open for 5% of the time, Pallas kernels for 23%

profile of v2, /device:TPU:0, one launch (start us, length us, event | category | flops | bytes accessed | tf_op | source)
XLA Modules:
  0.0 146.8 jit_solution(18217806694936892634)
XLA Ops:
  0.0 2.4 %collective-permute-start = (f32[3,8192]{1,0:T(4,128)}, f32[3,8192]{1,0:T(4,128)S(1)}, u32[]{:S(2)}, u32[]{:S(2)}) collective-permute-start(f32[3,8192]{1,0:T(4,128)} %own_ref.2), channel_id=1, source_target_pairs={{0,1},{1,2},{2,3},{3,4},{4,5},{5,6},{6,7},{7,8},{8,9},{9,10},{10,1... | collective-permute-start | bytes 294920 | tf_op jit(solution)/shard_map/ppermute | solution.py:208
  2.4 1.3 collective-permute-start.1
  3.7 0.7 reduce
  4.4 0.1 reshape.25.base_t_ref
  4.5 0.8 reshape.24.mid_t_ref
  5.3 1.3 reshape.22.basis_ref
  6.7 1.3 reshape.23.leaf_t_ref
  8.0 3.6 %upward.1 = bf16[64,128]{1,0:T(8,128)(2,1)S(1)} custom-call(bf16[2048,128]{1,0:T(8,128)(2,1)S(1)} %reshape.22.basis_ref, bf16[8192,128]{1,0:T(8,128)(2,1)} %own_ref.3, bf16[2048,32]{1,0:T(8,128)(2,1)S(1)} %reshape.23.leaf_t_ref, bf16[256,32]{1,0:T(8,128)(2,1)S(1)} %reshape.24.mid_t_ref, bf16[32,32]{1,0:T(8,128)(2,1)S(1)} %reshape.25.base_t_ref), custom_call_target="tpu_custom_call" | custom-call | flops 70000000 | bytes 3000000 | tf_op jit(solution)/shard_map/upward/pallas_call | solution.py:217
  11.6 46.7 %all_gather.3.all_ref = bf16[2048,128]{1,0:T(8,128)(2,1)S(1)} all-gather(bf16[64,128]{1,0:T(8,128)(2,1)S(1)} %upward.1), channel_id=1, replica_groups=mesh['leaf'=32] {'leaf'}, dimensions={0}, use_global_device_ids=true | all-gather | bytes 540672 | tf_op jit(solution)/shard_map/all_gather | solution.py:227
  58.2 0.7 copy-done.6
  58.9 0.6 copy-done.8
  59.6 1.3 collective-permute-start.3
  60.8 4.4 %collective-permute-start.2 = (bf16[8192,128]{1,0:T(8,128)(2,1)}, bf16[8192,128]{1,0:T(8,128)(2,1)}, u32[]{:S(2)}, u32[]{:S(2)}) collective-permute-start(bf16[8192,128]{1,0:T(8,128)(2,1)} %own_ref.3), channel_id=1, source_target_pairs={{0,1},{1,2},{2,3},{3,4},{4,5},{5,6},{6,7},{7,8},{8,9},{9,10},{10,1... | collective-permute-start | bytes 6291464 | tf_op jit(solution)/shard_map/ppermute | solution.py:231
  65.2 0.1 copy.17.near_ref
  65.3 0.1 reshape.21.top_blocks_ref
  65.4 2.2 %reshape.20.blocks_ref = bf16[6048,32]{1,0:T(8,128)(2,1)S(1)} reshape(bf16[189,1024]{1,0:T(8,128)(2,1)} %param.20) | data formatting | bytes 774144 | tf_op jit(solution)/shard_map/reshape | solution.py:250
  67.7 2.6 %couple.1 = bf16[2048,128]{1,0:T(8,128)(2,1)S(1)} custom-call(s32[189]{0:T(256)S(1)} %bitcast.5, s32[189]{0:T(256)S(1)} %copy-done.2, s32[8]{0:T(128)S(1)} %copy-done.3, s32[8]{0:T(128)S(1)} %copy-done.4, bf16[6048,32]{1,0:T(8,128)(2,1)S(1)} %reshape.20.blocks_ref, bf16[256,32]{1,0:T(8,128)(2,1)S(1)} %reshape.21.top_blocks_ref, ...), custom_call_target="tpu_custom_call" | custom-call | flops 50000000 | bytes 3000000 | tf_op jit(solution)/shard_map/couple/pallas_call | solution.py:235
  70.4 0.8 copy-done
  71.2 2.6 %all-to-all-start = ((bf16[32,64,128]{2,1,0:T(8,128)(2,1)}), bf16[32,64,128]{2,1,0:T(8,128)(2,1)S(1)}, u32[]{:S(2)}, u32[]{:S(2)}) async-start(bf16[32,64,128]{2,1,0:T(8,128)(2,1)} %bitcast.4), calls=%async_computation | async-start | bytes 1048576 | tf_op jit(solution)/shard_map/all_to_all | solution.py:255
  73.8 0.9 copy-done.7
  74.7 0.9 copy-done.9
  75.6 27.4 %make.1.kernel_ref = bf16[64,128,3456]{2,1,0:T(8,128)(2,1)} custom-call(s32[64,27]{1,0:T(8,128)S(1)} %copy.17.near_ref, f32[3,8192]{1,0:T(4,128)S(1)} %copy-done.7, f32[3,8192]{1,0:T(4,128)S(1)} %copy-done.5, f32[3,8192]{1,0:T(4,128)S(1)} %copy-done.9), custom_call_target="tpu_custom_call" | custom-call | flops 16000000000 | bytes 60000000 | tf_op jit(solution)/shard_map/make/pallas_call | solution.py:257
  103.0 11.9 %all-to-all-done = bf16[32,64,128]{2,1,0:T(8,128)(2,1)S(1)} async-done(((bf16[32,64,128]{2,1,0:T(8,128)(2,1)}), bf16[32,64,128]{2,1,0:T(8,128)(2,1)S(1)}, u32[]{:S(2)}, u32[]{:S(2)}) %all-to-all-start) | async-done | bytes 524320 | tf_op jit(solution)/shard_map/all_to_all | solution.py:255
  114.9 31.9 %use.1 = bf16[8192,128]{1,0:T(8,128)(2,1)} custom-call(s32[64,27]{1,0:T(8,128)S(1)} %copy.17.near_ref, bf16[64,128,3456]{2,1,0:T(8,128)(2,1)} %make.1.kernel_ref, bf16[8192,128]{1,0:T(8,128)(2,1)} %collective-permute-done.2.before_ref, bf16[8192,128]{1,0:T(8,128)(2,1)} %own_ref.3, bf16[8192,128]{1,0:T(8,128)(2,1)} %collective-permute-done.3.after_ref, ...), custom_call_target="tpu_custom_call" | custom-call | flops 8000000000 | bytes 66000000 | tf_op jit(solution)/shard_map/use/pallas_call | solution.py:274
  (23 shorter events, 0.1 us)
Async XLA Ops:
  0.0 58.2 %collective-permute-start = (f32[3,8192]{1,0:T(4,128)}, f32[3,8192]{1,0:T(4,128)S(1)}, u32[]{:S(2)}, u32[]{:S(2)}) collective-permute-start(f32[3,8192]{1,0:T(4,128)} %own_ref.2), channel_id=1, source_target_pairs={{0,1},{1,2},{2,3},{3,4},{4,5},{5,6},{6,7},{7,8},{8,9},{9,10},{10,1... | collective-permute-start | bytes 294920 | tf_op jit(solution)/shard_map/ppermute | solution.py:208
  2.4 56.5 %collective-permute-start.1 = (f32[3,8192]{1,0:T(4,128)}, f32[3,8192]{1,0:T(4,128)S(1)}, u32[]{:S(2)}, u32[]{:S(2)}) collective-permute-start(f32[3,8192]{1,0:T(4,128)} %own_ref.2), channel_id=1, source_target_pairs={{1,0},{2,1},{3,2},{4,3},{5,4},{6,5},{7,6},{8,7},{9,8},{10,9},{11,1... | collective-permute-start | bytes 294920 | tf_op jit(solution)/shard_map/ppermute | solution.py:209
  6.6 58.6 %copy-start.10 = (s32[64,27]{0,1:T(8,128)S(1)}, s32[64,27]{0,1:T(8,128)}, u32[]{:S(2)}) copy-start(s32[64,27]{0,1:T(8,128)} %param.15) | copy-start | bytes 20740
  6.6 58.7 %copy-start.11 = (bf16[8,1024]{1,0:T(8,128)(2,1)S(1)}, bf16[8,1024]{1,0:T(8,128)(2,1)}, u32[]{:S(2)}) copy-start(bf16[8,1024]{1,0:T(8,128)(2,1)} %param.23) | copy-start | bytes 49156
  11.5 56.2 %copy-start.1 = (s32[189,1]{0,1:T(1,128)S(1)}, s32[189,1]{0,1:T(1,128)}, u32[]{:S(2)}) copy-start(s32[189,1]{0,1:T(1,128)} %param.21) | copy-start | bytes 2272
  11.5 56.2 %copy-start.2 = (s32[189]{0:T(256)S(1)}, s32[189]{0:T(256)}, u32[]{:S(2)}) copy-start(s32[189]{0:T(256)} %source_ref.1) | copy-start | bytes 2272
  11.5 56.2 %copy-start.3 = (s32[8]{0:T(128)S(1)}, s32[8]{0:T(128)}, u32[]{:S(2)}) copy-start(s32[8]{0:T(128)} %top_target_ref.1) | copy-start | bytes 100
  11.6 56.2 %copy-start.4 = (s32[8]{0:T(128)S(1)}, s32[8]{0:T(128)}, u32[]{:S(2)}) copy-start(s32[8]{0:T(128)} %top_source_ref.1) | copy-start | bytes 100
  58.2 0.7 copy-start.6
  58.9 0.7 copy-start.8
  59.6 55.3 %collective-permute-start.3 = (bf16[8192,128]{1,0:T(8,128)(2,1)}, bf16[8192,128]{1,0:T(8,128)(2,1)}, u32[]{:S(2)}, u32[]{:S(2)}) collective-permute-start(bf16[8192,128]{1,0:T(8,128)(2,1)} %own_ref.3), channel_id=1, source_target_pairs={{1,0},{2,1},{3,2},{4,3},{5,4},{6,5},{7,6},{8,7},{9,8},{10,9},{11,1... | collective-permute-start | bytes 6291464 | tf_op jit(solution)/shard_map/ppermute | solution.py:232
  60.8 54.0 %collective-permute-start.2 = (bf16[8192,128]{1,0:T(8,128)(2,1)}, bf16[8192,128]{1,0:T(8,128)(2,1)}, u32[]{:S(2)}, u32[]{:S(2)}) collective-permute-start(bf16[8192,128]{1,0:T(8,128)(2,1)} %own_ref.3), channel_id=1, source_target_pairs={{0,1},{1,2},{2,3},{3,4},{4,5},{5,6},{6,7},{7,8},{8,9},{9,10},{10,1... | collective-permute-start | bytes 6291464 | tf_op jit(solution)/shard_map/ppermute | solution.py:231
  67.7 6.1 %copy-start.5 = (f32[3,8192]{1,0:T(4,128)S(1)}, f32[3,8192]{1,0:T(4,128)}, u32[]{:S(2)}) copy-start(f32[3,8192]{1,0:T(4,128)} %own_ref.2) | copy-start | bytes 294916
  70.4 0.8 copy-start
  71.2 43.7 %all-to-all-start = ((bf16[32,64,128]{2,1,0:T(8,128)(2,1)}), bf16[32,64,128]{2,1,0:T(8,128)(2,1)S(1)}, u32[]{:S(2)}, u32[]{:S(2)}) async-start(bf16[32,64,128]{2,1,0:T(8,128)(2,1)} %bitcast.4), calls=%async_computation | async-start | bytes 1048576 | tf_op jit(solution)/shard_map/all_to_all | solution.py:255
  73.8 0.9 copy-start.7
  74.7 0.9 copy-start.9
